TPU v7x, 8 devices: a whole 2x2x1 slice. The times are simulated.
8 devices in a mesh: dp: 2 (over z, y), tp: 4 (over x, core).
Axes of the slice: x: 2, y: 2, z: 1, core: 2. Of those that a mesh axis runs over, the one named last changes fastest.
Arguments:
- act_in: bfloat16 [512, 5120], P('dp'), parts along dimension 0
- w_qkv: bfloat16 [2, 5120, 40, 3, 128], P(None, None, 'tp')
- w_out: bfloat16 [2, 40, 128, 5120], P(None, 'tp')
- w_up: bfloat16 [2, 5120, 20480], P(None, None, 'tp')
- w_down: bfloat16 [2, 20480, 5120], P(None, 'tp')
- gain_one: float32 [2, 5120], replicated
- gain_two: float32 [2, 5120], replicated
Outputs:
- output: bfloat16 [512, 5120], P('dp'), parts along dimension 0
There are 2 independent parts. A program takes and returns all parts, laid end to end along the dimension named above; an argument that names none is the same for every part.
All inputs are finite; a program needn't handle non-finite values.
Results may differ from a plain program's by a relative error of at most 0.0152739.
Values are sent between devices in bfloat16 or wider.
A program may use at most 1.25 GiB of HBM per device.

v0:
```python
import math
import jax
import jax.numpy as jnp
from jax import lax
from jax.sharding import PartitionSpec as P


def layer_norm(act_rows, gain_vec):
    rows_f32 = act_rows.astype(jnp.float32)
    centred = rows_f32 - jnp.mean(rows_f32, axis=-1, keepdims=True)
    var_rows = jnp.mean(centred * centred, axis=-1, keepdims=True)
    return (centred * lax.rsqrt(var_rows + 1e-5) * gain_vec).astype(jnp.bfloat16)


def causal_attention(query_rows, key_rows, value_rows, query_start):
    n_q, num_heads, head_dim = query_rows.shape
    seq_k = key_rows.shape[0]
    limit_rows = max(8, 2 ** 24 // (num_heads * seq_k))
    row_block = math.gcd(n_q, 2 ** int(math.log2(limit_rows)))
    score_scale = 1.0 / math.sqrt(head_dim)
    key_pos = jnp.arange(seq_k)

    def one_block(blk_idx):
        row_start = blk_idx * row_block
        q_blk = lax.dynamic_slice_in_dim(query_rows, row_start, row_block, axis=0)
        scores = jnp.einsum("qhd,khd->hqk", q_blk, key_rows, preferred_element_type=jnp.float32) * score_scale
        q_pos = query_start + row_start + jnp.arange(row_block)
        scores = jnp.where(key_pos[None, None, :] <= q_pos[None, :, None], scores, -1e30)
        exp_scores = jnp.exp(scores - jnp.max(scores, axis=-1, keepdims=True))
        prob_sum = jnp.sum(exp_scores, axis=-1)
        mix_out = jnp.einsum("hqk,khd->qhd", exp_scores.astype(jnp.bfloat16), value_rows, preferred_element_type=jnp.float32)
        return (mix_out / prob_sum.T[:, :, None]).astype(jnp.bfloat16)

    blocks = lax.map(one_block, jnp.arange(n_q // row_block))
    return blocks.reshape(n_q, num_heads, head_dim)


def solution(mesh):
    def device_fn(act_in, w_qkv, w_out, w_up, w_down, gain_one, gain_two):
        act_rows = act_in
        for layer_idx in range(w_qkv.shape[0]):
            normed = layer_norm(act_rows, gain_one[layer_idx])
            qkv_rows = jnp.einsum("sm,mhcd->shcd", normed, w_qkv[layer_idx], preferred_element_type=jnp.float32).astype(jnp.bfloat16)
            attn_rows = causal_attention(qkv_rows[:, :, 0], qkv_rows[:, :, 1], qkv_rows[:, :, 2], 0)
            part_sum = jnp.einsum("shd,hdm->sm", attn_rows, w_out[layer_idx], preferred_element_type=jnp.float32).astype(jnp.bfloat16)
            attn_sum = lax.psum(part_sum, "tp")
            act_rows = (act_rows.astype(jnp.float32) + attn_sum.astype(jnp.float32)).astype(jnp.bfloat16)
            normed = layer_norm(act_rows, gain_two[layer_idx])
            hidden = jax.nn.gelu(jnp.dot(normed, w_up[layer_idx], preferred_element_type=jnp.float32), approximate=True).astype(jnp.bfloat16)
            part_sum = jnp.dot(hidden, w_down[layer_idx], preferred_element_type=jnp.float32).astype(jnp.bfloat16)
            mlp_sum = lax.psum(part_sum, "tp")
            act_rows = (act_rows.astype(jnp.float32) + mlp_sum.astype(jnp.float32)).astype(jnp.bfloat16)
        return act_rows

    return jax.shard_map(
        device_fn,
        mesh=mesh,
        in_specs=(
            P("dp", None),
            P(None, None, "tp", None, None),
            P(None, "tp", None, None),
            P(None, None, "tp"),
            P(None, "tp", None),
            P(None, None),
            P(None, None),
        ),
        out_specs=P("dp", None),
        check_vma=False,
    )
```

profile of v0, /device:TPU:0, one launch (start us, length us, event | category | flops | bytes accessed | tf_op | source)
XLA Modules:
  0.0 403.1 jit_solution(15564631048108072269)
XLA Ops:
  6.5 0.0 all-reduce.5.cloned.1.call-start
  6.6 0.0 copy-start.6
  6.6 2.3 convert_reduce_fusion.3
  8.9 0.1 copy-done
  9.1 0.8 fusion.59
  9.9 0.0 copy-done.6
  10.0 16.9 %fusion.114 = bf16[256,10,3,128]{3,0,2,1:T(8,128)(2,1)S(1)} fusion(bf16[2,5120,10,3,128]{4,1,3,2,0:T(8,128)(2,1)} %param.8, bf16[256,5120]{1,0:T(8,128)(2,1)S(1)} %copy-done, f32[5120]{0:T(1024)S(1)} %bitcast.127, f32[256]{0:T(256)S(1)} %add_rsqrt_fusion.3, f32[256]{0:T(256)S(1)} %broadcast_multiply_fusion.3), kind=kOutput, calls=%fused_computation.108 | convolution fusion | flops 10073866240 | bytes 43931648 | tf_op jit(solution)/shard_map/sm,mhcd->shcd/dot_general | solution.py:43
  26.8 0.0 copy-start.9
  26.8 0.5 fusion.108
  27.4 0.0 copy-start.5
  27.4 1.6 copy-done.5
  29.0 0.6 fusion.110
  29.5 0.0 copy-done.9
  29.5 10.1 %fusion.33 = bf16[256,5120]{1,0:T(8,128)(2,1)} fusion(bf16[2,10,128,5120]{3,2,1,0:T(8,128)(2,1)} %param.9, f32[10,256,256]{1,2,0:T(8,128)} %copy-done.5, f32[10,256]{1,0:T(8,128)S(1)} %get-tuple-element.50, pred[256,256]{0,1:T(8,128)(4,1)S(1)} %iota_compare_fusion, bf16[256,10,3,128]{3,0,2,1:T(8,128)(2,1)} %copy-done.9, f32[256,10]{0,1:T(8,128)S(1)} %bitcast.129), kind=kOutput, calls=%fused_computation.41 | convolution fusion | flops 3527802880 | bytes 19091456 | tf_op jit(solution)/shard_map/shd,hdm->sm/dot_general | solution.py:45
  39.6 0.0 all-reduce.5.cloned.1.call-update
  39.6 0.2 all-reduce.7.cloned.1.call-start
  39.9 0.5 copy-done.7
  40.4 56.4 %all-reduce.5.cloned.1.call-done = bf16[256,5120]{1,0:T(8,128)(2,1)} async-done(((bf16[256,5120]{1,0:T(8,128)(2,1)}), bf16[256,5120]{1,0:T(8,128)(2,1)}) %all-reduce.5.cloned.1.call-update) | async-done | bytes 2621456 | tf_op jit(solution)/shard_map/psum | solution.py:46
  96.8 2.8 convert_reduce_fusion.2
  99.6 0.0 copy-start.1
  99.6 0.8 fusion.56
  100.4 0.7 copy-done.1
  101.1 21.6 %fusion.73 = bf16[256,5120]{1,0:T(8,128)(2,1)S(1)} fusion(bf16[2,5120,5120]{2,1,0:T(8,128)(2,1)} %param.10, bf16[256,5120]{1,0:T(8,128)(2,1)S(1)} %get-tuple-element.38, f32[5120]{0:T(1024)S(1)} %bitcast.126, f32[256]{0:T(256)S(1)} %add_rsqrt_fusion.2, f32[256]{0:T(256)S(1)} %broadcast_multiply_fusion.2), kind=kOutput, calls=%fused_computation.73 | convolution fusion | flops 13440122880 | bytes 57694208 | tf_op jit(solution)/shard_map/dot_general | solution.py:49
  122.7 23.3 %fusion.36 = bf16[256,5120]{1,0:T(8,128)(2,1)} fusion(bf16[256,5120]{1,0:T(8,128)(2,1)S(1)} %fusion.73, bf16[2,5120,5120]{2,1,0:T(8,128)(2,1)} %param.11), kind=kOutput, calls=%fused_computation.42 | convolution fusion | flops 13423083520 | bytes 57671680 | tf_op jit(solution)/shard_map/dot_general | solution.py:50
  146.0 0.0 all-reduce.7.cloned.1.call-update
  146.0 0.3 all-reduce.9.cloned.1.call-start
  146.3 54.2 %all-reduce.7.cloned.1.call-done = bf16[256,5120]{1,0:T(8,128)(2,1)} async-done(((bf16[256,5120]{1,0:T(8,128)(2,1)}), bf16[256,5120]{1,0:T(8,128)(2,1)}) %all-reduce.7.cloned.1.call-update) | async-done | bytes 2621456 | tf_op jit(solution)/shard_map/psum | solution.py:51
  200.4 3.6 convert_reduce_fusion.1
  204.0 0.8 fusion.53
  204.9 16.9 %fusion.119 = bf16[256,10,3,128]{3,0,2,1:T(8,128)(2,1)S(1)} fusion(bf16[2,5120,10,3,128]{4,1,3,2,0:T(8,128)(2,1)} %param.8, bf16[256,5120]{1,0:T(8,128)(2,1)S(1)} %get-tuple-element.36, f32[5120]{0:T(1024)S(1)} %bitcast.125, f32[256]{0:T(256)S(1)} %add_rsqrt_fusion.1, f32[256]{0:T(256)S(1)} %broadcast_multiply_fusion.1), kind=kOutput, calls=%fused_computation.109 | convolution fusion | flops 10073866240 | bytes 43931648 | tf_op jit(solution)/shard_map/sm,mhcd->shcd/dot_general | solution.py:43
  221.8 0.0 copy-start.8
  221.8 0.5 fusion.109
  222.3 0.0 copy-start.4
  222.3 1.6 copy-done.4
  223.9 0.6 fusion.112
  224.5 10.1 %fusion.30 = bf16[256,5120]{1,0:T(8,128)(2,1)} fusion(bf16[2,10,128,5120]{3,2,1,0:T(8,128)(2,1)} %param.9, f32[10,256,256]{1,2,0:T(8,128)} %copy-done.4, f32[10,256]{1,0:T(8,128)S(1)} %get-tuple-element.53, pred[256,256]{0,1:T(8,128)(4,1)S(1)} %iota_compare_fusion, bf16[256,10,3,128]{3,0,2,1:T(8,128)(2,1)} %copy-done.8, f32[256,10]{0,1:T(8,128)S(1)} %bitcast.128), kind=kOutput, calls=%fused_computation.40 | convolution fusion | flops 3527802880 | bytes 19091456 | tf_op jit(solution)/shard_map/shd,hdm->sm/dot_general | solution.py:45
  234.5 0.0 all-reduce.9.cloned.1.call-update
  234.6 0.3 all-reduce.11.cloned.1.call-start
  234.9 54.1 %all-reduce.9.cloned.1.call-done = bf16[256,5120]{1,0:T(8,128)(2,1)} async-done(((bf16[256,5120]{1,0:T(8,128)(2,1)}), bf16[256,5120]{1,0:T(8,128)(2,1)}) %all-reduce.9.cloned.1.call-update) | async-done | bytes 2621456 | tf_op jit(solution)/shard_map/psum | solution.py:46
  289.0 2.8 convert_reduce_fusion
  291.8 0.0 copy-start.2
  291.8 0.8 fusion.50
  292.6 0.6 copy-done.2
  293.3 21.7 %fusion.87 = bf16[256,5120]{1,0:T(8,128)(2,1)S(1)} fusion(bf16[2,5120,5120]{2,1,0:T(8,128)(2,1)} %param.10, bf16[256,5120]{1,0:T(8,128)(2,1)S(1)} %get-tuple-element.28, f32[5120]{0:T(1024)S(1)} %bitcast.124, f32[256]{0:T(256)S(1)} %add_rsqrt_fusion, f32[256]{0:T(256)S(1)} %broadcast_multiply_fusion), kind=kOutput, calls=%fused_computation.83 | convolution fusion | flops 13440122880 | bytes 57694208 | tf_op jit(solution)/shard_map/dot_general | solution.py:49
  315.0 22.9 %fusion.39 = bf16[256,5120]{1,0:T(8,128)(2,1)} fusion(bf16[256,5120]{1,0:T(8,128)(2,1)S(1)} %fusion.87, bf16[2,5120,5120]{2,1,0:T(8,128)(2,1)} %param.11), kind=kOutput, calls=%fused_computation.43 | convolution fusion | flops 13423083520 | bytes 57671680 | tf_op jit(solution)/shard_map/dot_general | solution.py:50
  338.0 0.0 all-reduce.11.cloned.1.call-update
  338.0 54.4 %all-reduce.11.cloned.1.call-done = bf16[256,5120]{1,0:T(8,128)(2,1)} async-done(((bf16[256,5120]{1,0:T(8,128)(2,1)}), bf16[256,5120]{1,0:T(8,128)(2,1)}) %all-reduce.11.cloned.1.call-update) | async-done | bytes 2621456 | tf_op jit(solution)/shard_map/psum | solution.py:51
  392.4 4.2 %fusion.77 = bf16[256,5120]{1,0:T(8,128)(2,1)} fusion(bf16[256,5120]{1,0:T(8,128)(2,1)S(1)} %copy-done.3, bf16[256,5120]{1,0:T(8,128)(2,1)} %all-reduce.11.cloned.1.call-done), kind=kLoop, calls=%fused_computation.75 | loop fusion | flops 5242880 | bytes 7864320 | tf_op jit(solution)/shard_map/convert_element_type | solution.py:52
  (16 shorter events, 0.2 us)
Async XLA Ops:
  6.5 2.5 copy-start
  6.5 90.3 %all-reduce.5.cloned.1.call-start = ((), (), s32[]{:S(2)}) async-start(), calls=%async_computation | async-start | bytes 5242880 | tf_op jit(solution)/shard_map/psum | solution.py:46
  6.6 3.3 copy-start.6
  26.8 2.7 copy-start.9
  27.4 1.6 copy-start.5
  39.6 0.8 copy-start.7
  39.6 160.8 %all-reduce.7.cloned.1.call-start = ((), (), s32[]{:S(2)}) async-start(), calls=%async_computation.1 | async-start | bytes 5242880 | tf_op jit(solution)/shard_map/psum | solution.py:51
  99.6 1.5 copy-start.1
  146.0 143.0 %all-reduce.9.cloned.1.call-start = ((), (), s32[]{:S(2)}) async-start(), calls=%async_computation.2 | async-start | bytes 5242880 | tf_op jit(solution)/shard_map/psum | solution.py:46
  221.8 2.7 copy-start.8
  222.3 1.6 copy-start.4
  234.6 157.8 %all-reduce.11.cloned.1.call-start = ((), (), s32[]{:S(2)}) async-start(), calls=%async_computation.3 | async-start | bytes 5242880 | tf_op jit(solution)/shard_map/psum | solution.py:51
  291.8 1.5 copy-start.2
  337.9 54.5 %copy-start.3 = (bf16[256,5120]{1,0:T(8,128)(2,1)S(1)}, bf16[256,5120]{1,0:T(8,128)(2,1)}, u32[]{:S(2)}) copy-start(bf16[256,5120]{1,0:T(8,128)(2,1)} %copy-done.2) | copy-start | bytes 7864324
Sparse Core Ops, SparseCore 0:
  39.8 56.9 all-reduce.4
  146.1 54.2 all-reduce.6
  234.7 54.2 all-reduce.8
  338.1 54.2 all-reduce.10
where the time goes:
time: 404 us; the launch traced here: 403 us
  waiting for transfers between devices  219 us (54%)
  matrix products  145 us (36%)
  other arithmetic  20.1 us (5%)
  between operations  13.3 us (3%)
  local copies, waits for them, and re-layouts  5.21 us (1%)
    psum x2, waiting for transfers between devices, device_fn(): attn_sum = lax.psum(part_sum, 'tp')  110 us
    psum x2, waiting for transfers between devices, device_fn(): mlp_sum = lax.psum(part_sum, 'tp')  109 us
    dot_general x2, matrix products, device_fn(): jnp.dot(hidden, w_down[layer_idx], preferred_element_type=jnp.float32)  46.2 us
    dot_general x2, matrix products, device_fn(): jnp.dot(normed, w_up[layer_idx], preferred_element_type=jnp.float32)  43.3 us
    dot_general x2, matrix products, device_fn(): jnp.einsum('sm,mhcd->shcd', normed, w_qkv[layer_idx], preferred_element_t...  33.8 us
    dot_general x2, matrix products, device_fn(): jnp.einsum('shd,hdm->sm', attn_rows, w_out[layer_idx], preferred_element_...  20.2 us
    reduce_sum x4, other arithmetic, layer_norm(): centred = rows_f32 - jnp.mean(rows_f32, axis=-1, keepdims=True)  11.4 us
  transfers between devices with their start and end apart: 4, of which 4 were waited for; matrix products, arithmetic and copies ran while one was open for 0% of the time, Pallas kernels for 0%

commit v1 on v0

v1 whole, which is shorter than its diff:
```python
import functools
import math
import jax
import jax.numpy as jnp
from jax import lax
from jax.experimental import pallas as pl
from jax.experimental.pallas import tpu as pltpu
from jax.sharding import PartitionSpec as P

MESH = pl.DeviceIdType.MESH
F32, BF16 = jnp.float32, jnp.bfloat16
WID = 512
LAG_X = 4
LAG_USE = 5
A_SLOTS, B_SLOTS, C_SLOTS = 3, 3, 4


def layer_kernel(
    num_layers, seq, dim, heads, hd, ffn,
    x_hbm, wqkv, wo, w1, w2, g1_ref, g2_ref, out_hbm,
    xs, acc, hid, part, recv_a, send_c, recv_c, ys, mean0, sum1, sum2,
    a_buf, b_buf, c_buf,
    x_sem, a_sem, b_sem, c_sem, o_sem, sa, ra, sc, rc, sd, rd,
):
    dp = lax.axis_index("dp")
    tp = lax.axis_index("tp")
    core = lax.rem(tp, 2)
    sib = (dp, tp + 1 - 2 * core)
    pair = (dp, lax.rem(tp + 2, 4))
    half = seq // 2
    mine = pl.ds(pl.multiple_of(core * half, half), half)
    other = pl.ds(pl.multiple_of((1 - core) * half, half), half)
    nc = dim // WID
    qkv_tiles, up_tiles = heads * 3 * hd // 256, ffn // 256
    o_off = heads * 3 * hd

    barrier = pltpu.get_barrier_semaphore()
    for peer in (sib, pair):
        pl.semaphore_signal(barrier, inc=1, device_id=peer, device_id_type=MESH)
    pl.semaphore_wait(barrier, 2)

    def rows(j):
        return pl.ds(pl.multiple_of(j * WID, WID), WID)

    def x_copy(j):
        return pltpu.make_async_copy(x_hbm.at[:, rows(j)], xs.at[j], x_sem.at[j])

    def out_copy(j):
        return pltpu.make_async_copy(xs.at[j], out_hbm.at[:, rows(j)], o_sem.at[j])

    def a_start(stage, j):
        layer, is_up = stage // 2, stage % 2
        if stage >= 2 * num_layers:
            return
        slot = lax.rem(stage * nc + j, A_SLOTS)
        if is_up:
            def one(t, carry):
                cols = pl.ds(pl.multiple_of(t * 256, 256), 256)
                pltpu.make_async_copy(
                    w1.at[layer, rows(j), cols], a_buf.at[slot, t], a_sem.at[slot]
                ).start()
                return carry
            lax.fori_loop(0, up_tiles, one, 0)
        else:
            for s in range(2):
                pltpu.make_async_copy(
                    wqkv.at[layer, :, s, rows(j), :],
                    a_buf.at[slot, pl.ds(0, qkv_tiles), :, pl.ds(s * 128, 128)],
                    a_sem.at[slot],
                ).start()

    def a_next(stage, j):
        @pl.when(j + A_SLOTS < nc)
        def _():
            a_start(stage, j + A_SLOTS)

        @pl.when(j + A_SLOTS >= nc)
        def _():
            a_start(stage + 1, j + A_SLOTS - nc)

    def a_wait(stage, j):
        slot = lax.rem(stage * nc + j, A_SLOTS)
        tiles = up_tiles if stage % 2 else qkv_tiles
        view = a_buf.at[slot, pl.ds(0, tiles)]
        pltpu.make_async_copy(view, view, a_sem.at[slot]).wait()
        return slot

    def b_copy(layer, j):
        slot = lax.rem(layer * nc + j, B_SLOTS)
        return slot, pltpu.make_async_copy(
            w2.at[layer, :, rows(j)], b_buf.at[slot], b_sem.at[slot])

    def c_copy(layer, j):
        slot = lax.rem(layer * nc + j, C_SLOTS)
        return slot, pltpu.make_async_copy(
            wo.at[layer, :, rows(j)], c_buf.at[slot], c_sem.at[slot])

    def ring_next(copy, slots, layer, j):
        @pl.when(j + slots < nc)
        def _():
            copy(layer, j + slots)[1].start()

        if layer + 1 < num_layers:
            @pl.when(j + slots >= nc)
            def _():
                copy(layer + 1, j + slots - nc)[1].start()

    def use(stage, j):
        layer, is_up = stage // 2, stage % 2
        gain_ref = g2_ref if is_up else g1_ref
        gain = gain_ref[pl.ds(layer, 1), rows(j)]
        xc = xs[j].astype(F32)

        @pl.when(j == 0)
        def _():
            m = jnp.mean(xc, axis=1, keepdims=True)
            mean0[...] = jnp.broadcast_to(m, mean0.shape)
            sum1[...] = jnp.zeros_like(sum1)
            sum2[...] = jnp.zeros_like(sum2)
            acc[...] = jnp.zeros_like(acc)

        shift = mean0[...]
        s1, s2 = sum1[...], sum2[...]
        for t in range(WID // 128):
            cols = slice(t * 128, (t + 1) * 128)
            d = xs[j, :, cols].astype(F32) - shift
            s1 = s1 + d
            s2 = s2 + d * d
            ys[0:seq, cols] = (d * gain[:, cols]).astype(BF16)
        sum1[...] = s1
        sum2[...] = s2
        g_hi = gain.astype(BF16)
        g_lo = (gain - g_hi.astype(F32)).astype(BF16)
        row = lax.broadcasted_iota(jnp.int32, (16, WID), 0)
        hi = jnp.broadcast_to(g_hi.astype(F32), (16, WID))
        lo = jnp.broadcast_to(g_lo.astype(F32), (16, WID))
        extra = jnp.where(row == 0, hi, jnp.where(row == 1, lo, 0.0))
        ys[seq:seq + 16, :] = extra.astype(BF16)

        slot = a_wait(stage, j)
        lhs = ys[...]
        for t in range(up_tiles if is_up else qkv_tiles):
            cols = slice(t * 256, (t + 1) * 256)
            acc[:, cols] += jnp.dot(lhs, a_buf[slot, t], preferred_element_type=F32)
        a_next(stage, j)

    def use_end(stage):
        is_up = stage % 2
        delta = jnp.sum(sum1[...], axis=1, keepdims=True) * (1.0 / dim)
        var = jnp.sum(sum2[...], axis=1, keepdims=True) * (1.0 / dim) - delta * delta
        rstd = lax.rsqrt(jnp.maximum(var, 0.0) + 1e-5)

        def one(t, carry):
            cols = pl.ds(pl.multiple_of(t * 256, 256), 256)
            colsum = acc[seq:seq + 1, cols] + acc[seq + 1:seq + 2, cols]
            val = (acc[0:seq, cols] - delta * colsum) * rstd
            if is_up:
                val = jax.nn.gelu(val, approximate=True)
            hid[:, cols] = val.astype(BF16)
            return carry

        lax.fori_loop(0, up_tiles if is_up else qkv_tiles, one, 0)

    def attention():
        q_pos = lax.broadcasted_iota(jnp.int32, (seq, seq), 0)
        k_pos = lax.broadcasted_iota(jnp.int32, (seq, seq), 1)
        keep = k_pos <= q_pos
        scale = 1.0 / math.sqrt(hd)
        for h in range(heads):
            base = 3 * h * hd
            q = hid[:, base:base + hd]
            k = hid[:, base + hd:base + 2 * hd]
            v = hid[:, base + 2 * hd:base + 3 * hd]
            s = lax.dot_general(q, k, (((1,), (1,)), ((), ())), preferred_element_type=F32) * scale
            s = jnp.where(keep, s, -1e30)
            e = jnp.exp(s - jnp.max(s, axis=1, keepdims=True))
            total = jnp.sum(e, axis=1, keepdims=True)
            mix = jnp.dot(e.astype(BF16), v, preferred_element_type=F32)
            hid[:, o_off + h * hd:o_off + (h + 1) * hd] = (mix / total).astype(BF16)

    def make_out(layer, j):
        slot, copy = c_copy(layer, j)
        copy.wait()
        part[j] = jnp.dot(hid[:, o_off:], c_buf[slot], preferred_element_type=F32).astype(BF16)
        ring_next(c_copy, C_SLOTS, layer, j)

    def make_down(layer, j):
        slot, copy = b_copy(layer, j)
        copy.wait()
        part[j] = jnp.dot(hid[...], b_buf[slot], preferred_element_type=F32).astype(BF16)
        ring_next(b_copy, B_SLOTS, layer, j)

    def window(index, make, consume):
        par = index % 2

        def a_send(j):
            return pltpu.make_async_remote_copy(
                part.at[j, other], recv_a.at[par, j], sa.at[j], ra.at[par, j],
                device_id=sib, device_id_type=MESH)

        def c_send(j):
            return pltpu.make_async_remote_copy(
                send_c.at[j], recv_c.at[par, j], sc.at[j], rc.at[par, j],
                device_id=pair, device_id_type=MESH)

        def d_send(j):
            return pltpu.make_async_remote_copy(
                xs.at[j, mine], xs.at[j, mine], sd.at[j], rd.at[par, j],
                device_id=sib, device_id_type=MESH)

        def d_recv(j):
            return pltpu.make_async_remote_copy(
                xs.at[j, other], xs.at[j, other], sd.at[j], rd.at[par, j],
                device_id=sib, device_id_type=MESH)

        def step(i, carry):
            @pl.when(i < nc)
            def _():
                make(i)
                a_send(i).start()

            @pl.when(jnp.logical_and(i >= 1, i < nc + 1))
            def _():
                j = i - 1
                a_send(j).wait_recv()
                send_c[j] = (part[j, mine, :].astype(F32) + recv_a[par, j].astype(F32)).astype(BF16)
                c_send(j).start()

            @pl.when(jnp.logical_and(i >= LAG_X, i < nc + LAG_X))
            def _():
                j = i - LAG_X
                c_send(j).wait_recv()
                total = send_c[j].astype(F32) + recv_c[par, j].astype(F32)
                xs[j, mine, :] = (xs[j, mine, :].astype(F32) + total).astype(BF16)
                d_send(j).start()

            @pl.when(i >= LAG_USE)
            def _():
                j = i - LAG_USE
                a_send(j).wait_send()
                c_send(j).wait_send()
                d_send(j).wait_send()
                d_recv(j).wait_recv()
                consume(j)
            return carry

        lax.fori_loop(0, nc + LAG_USE, step, 0)

    for j in range(nc):
        x_copy(j).start()
    for j in range(A_SLOTS):
        a_start(0, j)

    def first(j, carry):
        x_copy(j).wait()
        use(0, j)
        return carry

    lax.fori_loop(0, nc, first, 0)
    for j in range(C_SLOTS):
        c_copy(0, j)[1].start()
    use_end(0)
    attention()
    for j in range(B_SLOTS):
        b_copy(0, j)[1].start()

    for layer in range(num_layers):
        window(2 * layer, functools.partial(make_out, layer), functools.partial(use, 2 * layer + 1))
        use_end(2 * layer + 1)
        if layer + 1 < num_layers:
            window(2 * layer + 1, functools.partial(make_down, layer), functools.partial(use, 2 * layer + 2))
            use_end(2 * layer + 2)
            attention()
        else:
            window(2 * layer + 1, functools.partial(make_down, layer), lambda j: out_copy(j).start())

    def last(j, carry):
        out_copy(j).wait()
        return carry

    lax.fori_loop(0, nc, last, 0)


def solution(mesh):
    def device_fn(act_in, w_qkv, w_out, w_up, w_down, gain_one, gain_two):
        seq, dim = act_in.shape
        num_layers, _, heads, _, hd = w_qkv.shape
        ffn = w_up.shape[2]
        nc = dim // WID
        wq = jnp.transpose(w_qkv, (0, 2, 3, 1, 4)).reshape(num_layers, heads * 3 // 2, 2, dim, hd)
        wo = w_out.reshape(num_layers, heads * hd, dim)
        any_spec = pl.BlockSpec(memory_space=pl.ANY)
        vmem_spec = pl.BlockSpec(memory_space=pltpu.VMEM)
        return pl.pallas_call(
            functools.partial(layer_kernel, num_layers, seq, dim, heads, hd, ffn),
            out_shape=jax.ShapeDtypeStruct((seq, dim), BF16),
            in_specs=[any_spec] * 5 + [vmem_spec] * 2,
            out_specs=any_spec,
            scratch_shapes=[
                pltpu.VMEM((nc, seq, WID), BF16),
                pltpu.VMEM((seq + 16, ffn), F32),
                pltpu.VMEM((seq, ffn), BF16),
                pltpu.VMEM((nc, seq, WID), BF16),
                pltpu.VMEM((2, nc, seq // 2, WID), BF16),
                pltpu.VMEM((nc, seq // 2, WID), BF16),
                pltpu.VMEM((2, nc, seq // 2, WID), BF16),
                pltpu.VMEM((seq + 16, WID), BF16),
                pltpu.VMEM((seq, 128), F32),
                pltpu.VMEM((seq, 128), F32),
                pltpu.VMEM((seq, 128), F32),
                pltpu.VMEM((A_SLOTS, ffn // 256, WID, 256), BF16),
                pltpu.VMEM((B_SLOTS, ffn, WID), BF16),
                pltpu.VMEM((C_SLOTS, heads * hd, WID), BF16),
                pltpu.SemaphoreType.DMA((nc,)),
                pltpu.SemaphoreType.DMA((A_SLOTS,)),
                pltpu.SemaphoreType.DMA((B_SLOTS,)),
                pltpu.SemaphoreType.DMA((C_SLOTS,)),
                pltpu.SemaphoreType.DMA((nc,)),
                pltpu.SemaphoreType.DMA((nc,)),
                pltpu.SemaphoreType.DMA((2, nc)),
                pltpu.SemaphoreType.DMA((nc,)),
                pltpu.SemaphoreType.DMA((2, nc)),
                pltpu.SemaphoreType.DMA((nc,)),
                pltpu.SemaphoreType.DMA((2, nc)),
            ],
            compiler_params=pltpu.CompilerParams(
                collective_id=0, has_side_effects=True, vmem_limit_bytes=67_000_000),
            name="layers",
        )(act_in, wq, wo, w_up, w_down, gain_one, gain_two)

    return jax.shard_map(
        device_fn,
        mesh=mesh,
        in_specs=(
            P("dp", None),
            P(None, None, "tp", None, None),
            P(None, "tp", None, None),
            P(None, None, "tp"),
            P(None, "tp", None),
            P(None, None),
            P(None, None),
        ),
        out_specs=P("dp", None),
        check_vma=False,
    )
```

time: 404 us -> 180 us (0.45)
  waiting for transfers between devices: 219 us -> 0 us
  Pallas kernels: 0 us -> 176 us
  matrix products: 145 us -> 0 us
  other arithmetic: 20.1 us -> 0 us
  between operations: 13.3 us -> 0.01 us
    psum x4 -> x0, waiting for transfers between devices: 219 us -> none  [the longest x2 110 us: device_fn(): attn_sum = lax.psum(part_sum, 'tp')]
    pallas_call x0 -> x1, Pallas kernels: none -> 176 us  [device_fn(): pl.pallas_call(functools.partial(layer_kernel, num_layers, seq, dim, head...]
    dot_general x10 -> x0, matrix products: 145 us -> none  [the longest x2 46.2 us: device_fn(): jnp.dot(hidden, w_down[layer_idx], preferred_element_type=jnp.float32)]
    reduce_sum x10 -> x0, other arithmetic: 15.8 us -> none  [the longest x4 11.4 us: layer_norm(): centred = rows_f32 - jnp.mean(rows_f32, axis=-1, keepdims=True)]
    convert_element_type x1 -> x0, other arithmetic: 4.2 us -> none  [device_fn(): (act_rows.astype(jnp.float32) + mlp_sum.astype(jnp.float32)).astype(jnp.b...]
  transfers between devices with their start and end apart: 4 -> 0, of which waited for: 4 -> 0; matrix products, arithmetic and copies ran while one was open for 0% -> 0% of each run, Pallas kernels for 0% -> 0%
where the time goes in v1:
time: 180 us; the launch traced here: 179 us
  Pallas kernels  176 us (98%)
  local copies, waits for them, and re-layouts  3.4 us (2%)
    pallas_call x1, Pallas kernels, device_fn(): pl.pallas_call(functools.partial(layer_kernel, num_layers, seq, dim, head...  176 us

profile of v1, /device:TPU:0, one launch (start us, length us, event | category | flops | bytes accessed | tf_op | source)
XLA Modules:
  0.0 179.4 jit_solution(13938882993867047238)
XLA Ops:
  0.0 175.9 %layers.1 = bf16[256,5120]{1,0:T(8,128)(2,1)} custom-call(bf16[256,5120]{1,0:T(8,128)(2,1)} %x_hbm.1, bf16[2,15,2,5120,128]{4,3,2,1,0:T(8,128)(2,1)} %bitcast.1.wqkv, bf16[2,1280,5120]{2,1,0:T(8,128)(2,1)} %bitcast.4, bf16[2,5120,5120]{2,1,0:T(8,128)(2,1)} %w1.1, bf16[2,5120,5120]{2,1,0:T(8,128)(2,1)} %w2.1, f32[2,5120]{1,0:T(2,128)} %g1_ref.1, f32[2,5120]{1,0:T(2,128)} %g2_ref.1), custom_call_target="tpu_custom_call" | custom-call | tf_op jit(solution)/shard_map/layers/pallas_call | solution.py:294
  176.0 3.4 %copy.9 = bf16[256,5120]{1,0:T(8,128)(2,1)} copy(bf16[256,5120]{1,0:T(8,128)(2,1)} %layers.1) | data formatting | bytes 5242880

commit v2 on v1

--- a/solution.py
+++ b/solution.py
@@ -10,17 +10,20 @@
 MESH = pl.DeviceIdType.MESH
 F32, BF16 = jnp.float32, jnp.bfloat16
 WID = 512
+GAIN = 16
 LAG_X = 4
 LAG_USE = 5
+GELU_A = math.sqrt(2.0 / math.pi)
+GELU_B = 0.044715 * GELU_A
 A_SLOTS, B_SLOTS, C_SLOTS = 3, 3, 4
 
 
 def layer_kernel(
     num_layers, seq, dim, heads, hd, ffn,
-    x_hbm, wqkv, wo, w1, w2, g1_ref, g2_ref, out_hbm,
-    xs, acc, hid, part, recv_a, send_c, recv_c, ys, mean0, sum1, sum2,
+    x_hbm, wqkv, wo, w1, w2, g1_hbm, g2_hbm, out_hbm,
+    g1_ref, g2_ref, xs, acc, hid, part, recv_a, send_c, recv_c, ys0, ys1, mean0, sum1, sum2,
     a_buf, b_buf, c_buf,
-    x_sem, a_sem, b_sem, c_sem, o_sem, sa, ra, sc, rc, sd, rd,
+    g_sem, x_sem, a_sem, b_sem, c_sem, o_sem, sa, ra, sc, rc, sd, rd,
 ):
     dp = lax.axis_index("dp")
     tp = lax.axis_index("tp")
@@ -37,7 +40,6 @@
     barrier = pltpu.get_barrier_semaphore()
     for peer in (sib, pair):
         pl.semaphore_signal(barrier, inc=1, device_id=peer, device_id_type=MESH)
-    pl.semaphore_wait(barrier, 2)
 
     def rows(j):
         return pl.ds(pl.multiple_of(j * WID, WID), WID)
@@ -58,7 +60,7 @@
                 cols = pl.ds(pl.multiple_of(t * 256, 256), 256)
                 pltpu.make_async_copy(
                     w1.at[layer, rows(j), cols], a_buf.at[slot, t], a_sem.at[slot]
-                ).start()
+                ).start(priority=1)
                 return carry
             lax.fori_loop(0, up_tiles, one, 0)
         else:
@@ -67,7 +69,7 @@
                     wqkv.at[layer, :, s, rows(j), :],
                     a_buf.at[slot, pl.ds(0, qkv_tiles), :, pl.ds(s * 128, 128)],
                     a_sem.at[slot],
-                ).start()
+                ).start(priority=1)
 
     def a_next(stage, j):
         @pl.when(j + A_SLOTS < nc)
@@ -95,30 +97,26 @@
         return slot, pltpu.make_async_copy(
             wo.at[layer, :, rows(j)], c_buf.at[slot], c_sem.at[slot])
 
-    def ring_next(copy, slots, layer, j):
+    def ring_next(copy, slots, priority, layer, j):
         @pl.when(j + slots < nc)
         def _():
-            copy(layer, j + slots)[1].start()
+            copy(layer, j + slots)[1].start(priority=priority)
 
         if layer + 1 < num_layers:
             @pl.when(j + slots >= nc)
             def _():
-                copy(layer + 1, j + slots - nc)[1].start()
-
-    def use(stage, j):
+                copy(layer + 1, j + slots - nc)[1].start(priority=priority)
+
+    def prep_start(j):
+        m = jnp.mean(xs[j].astype(F32), axis=1, keepdims=True)
+        mean0[...] = jnp.broadcast_to(m, mean0.shape)
+        sum1[...] = jnp.zeros_like(sum1)
+        sum2[...] = jnp.zeros_like(sum2)
+
+    def prep(stage, j, y_ref):
         layer, is_up = stage // 2, stage % 2
         gain_ref = g2_ref if is_up else g1_ref
         gain = gain_ref[pl.ds(layer, 1), rows(j)]
-        xc = xs[j].astype(F32)
-
-        @pl.when(j == 0)
-        def _():
-            m = jnp.mean(xc, axis=1, keepdims=True)
-            mean0[...] = jnp.broadcast_to(m, mean0.shape)
-            sum1[...] = jnp.zeros_like(sum1)
-            sum2[...] = jnp.zeros_like(sum2)
-            acc[...] = jnp.zeros_like(acc)
-
         shift = mean0[...]
         s1, s2 = sum1[...], sum2[...]
         for t in range(WID // 128):
@@ -126,40 +124,58 @@
             d = xs[j, :, cols].astype(F32) - shift
             s1 = s1 + d
             s2 = s2 + d * d
-            ys[0:seq, cols] = (d * gain[:, cols]).astype(BF16)
+            y_ref[GAIN:, cols] = (d * gain[:, cols]).astype(BF16)
         sum1[...] = s1
         sum2[...] = s2
         g_hi = gain.astype(BF16)
         g_lo = (gain - g_hi.astype(F32)).astype(BF16)
-        row = lax.broadcasted_iota(jnp.int32, (16, WID), 0)
-        hi = jnp.broadcast_to(g_hi.astype(F32), (16, WID))
-        lo = jnp.broadcast_to(g_lo.astype(F32), (16, WID))
+        row = lax.broadcasted_iota(jnp.int32, (GAIN, WID), 0)
+        hi = jnp.broadcast_to(g_hi.astype(F32), (GAIN, WID))
+        lo = jnp.broadcast_to(g_lo.astype(F32), (GAIN, WID))
         extra = jnp.where(row == 0, hi, jnp.where(row == 1, lo, 0.0))
-        ys[seq:seq + 16, :] = extra.astype(BF16)
-
-        slot = a_wait(stage, j)
-        lhs = ys[...]
-        for t in range(up_tiles if is_up else qkv_tiles):
+        y_ref[0:GAIN, :] = extra.astype(BF16)
+
+    def mul(stage, slot, y_ref):
+        lhs = y_ref[...]
+        for t in range(up_tiles if stage % 2 else qkv_tiles):
             cols = slice(t * 256, (t + 1) * 256)
             acc[:, cols] += jnp.dot(lhs, a_buf[slot, t], preferred_element_type=F32)
-        a_next(stage, j)
-
-    def use_end(stage):
+
+    def mul_last(stage, slot, y_ref):
         is_up = stage % 2
         delta = jnp.sum(sum1[...], axis=1, keepdims=True) * (1.0 / dim)
         var = jnp.sum(sum2[...], axis=1, keepdims=True) * (1.0 / dim) - delta * delta
         rstd = lax.rsqrt(jnp.maximum(var, 0.0) + 1e-5)
-
-        def one(t, carry):
-            cols = pl.ds(pl.multiple_of(t * 256, 256), 256)
-            colsum = acc[seq:seq + 1, cols] + acc[seq + 1:seq + 2, cols]
-            val = (acc[0:seq, cols] - delta * colsum) * rstd
+        back = delta * rstd
+        lhs = y_ref[...]
+        for t in range(up_tiles if is_up else qkv_tiles):
+            cols = slice(t * 256, (t + 1) * 256)
+            full = acc[:, cols] + jnp.dot(lhs, a_buf[slot, t], preferred_element_type=F32)
+            colsum = full[0:1] + full[1:2]
+            val = full[GAIN:] * rstd - back * colsum
             if is_up:
-                val = jax.nn.gelu(val, approximate=True)
+                inner = val * (GELU_A + GELU_B * (val * val))
+                hv = 0.5 * val
+                val = hv + hv * jnp.tanh(inner)
             hid[:, cols] = val.astype(BF16)
-            return carry
-
-        lax.fori_loop(0, up_tiles if is_up else qkv_tiles, one, 0)
+
+    def use(stage, j):
+        @pl.when(j == 0)
+        def _():
+            prep_start(j)
+
+        prep(stage, j, ys0)
+        slot = a_wait(stage, j)
+
+        @pl.when(j < nc - 1)
+        def _():
+            mul(stage, slot, ys0)
+
+        @pl.when(j == nc - 1)
+        def _():
+            mul_last(stage, slot, ys0)
+
+        a_next(stage, j)
 
     def attention():
         q_pos = lax.broadcasted_iota(jnp.int32, (seq, seq), 0)
@@ -182,15 +198,15 @@
         slot, copy = c_copy(layer, j)
         copy.wait()
         part[j] = jnp.dot(hid[:, o_off:], c_buf[slot], preferred_element_type=F32).astype(BF16)
-        ring_next(c_copy, C_SLOTS, layer, j)
+        ring_next(c_copy, C_SLOTS, 0, layer, j)
 
     def make_down(layer, j):
         slot, copy = b_copy(layer, j)
         copy.wait()
         part[j] = jnp.dot(hid[...], b_buf[slot], preferred_element_type=F32).astype(BF16)
-        ring_next(b_copy, B_SLOTS, layer, j)
-
-    def window(index, make, consume):
+        ring_next(b_copy, B_SLOTS, 1, layer, j)
+
+    def window(index, make, consume, zero_acc=True):
         par = index % 2
 
         def a_send(j):
@@ -213,18 +229,26 @@
                 xs.at[j, other], xs.at[j, other], sd.at[j], rd.at[par, j],
                 device_id=sib, device_id_type=MESH)
 
+        def pair_sum(j):
+            a_send(j).wait_recv()
+            send_c[j] = (part[j, mine, :].astype(F32) + recv_a[par, j].astype(F32)).astype(BF16)
+            c_send(j).start()
+
         def step(i, carry):
             @pl.when(i < nc)
             def _():
                 make(i)
                 a_send(i).start()
 
-            @pl.when(jnp.logical_and(i >= 1, i < nc + 1))
-            def _():
-                j = i - 1
-                a_send(j).wait_recv()
-                send_c[j] = (part[j, mine, :].astype(F32) + recv_a[par, j].astype(F32)).astype(BF16)
-                c_send(j).start()
+            @pl.when(i == 0)
+            def _():
+                if zero_acc:
+                    acc[...] = jnp.zeros_like(acc)
+                pair_sum(0)
+
+            @pl.when(jnp.logical_and(i >= 2, i < nc + 1))
+            def _():
+                pair_sum(i - 1)
 
             @pl.when(jnp.logical_and(i >= LAG_X, i < nc + LAG_X))
             def _():
@@ -246,33 +270,53 @@
 
         lax.fori_loop(0, nc + LAG_USE, step, 0)
 
-    for j in range(nc):
+    x_copy(0).start()
+    g_copies = [pltpu.make_async_copy(src, dst, g_sem.at[n])
+                for n, (src, dst) in enumerate(((g1_hbm, g1_ref), (g2_hbm, g2_ref)))]
+    for copy in g_copies:
+        copy.start()
+    a_start(0, 0)
+    for j in range(1, nc):
         x_copy(j).start()
-    for j in range(A_SLOTS):
+    for j in range(1, A_SLOTS):
         a_start(0, j)
-
-    def first(j, carry):
-        x_copy(j).wait()
-        use(0, j)
+    acc[...] = jnp.zeros_like(acc)
+    for copy in g_copies:
+        copy.wait()
+    x_copy(0).wait()
+    prep_start(0)
+    prep(0, 0, ys0)
+
+    def first(j, now, then):
+        x_copy(j + 1).wait()
+        slot = a_wait(0, j)
+        prep(0, j + 1, then)
+        mul(0, slot, now)
+        a_next(0, j)
+
+    def first_two(i, carry):
+        first(2 * i, ys0, ys1)
+        first(2 * i + 1, ys1, ys0)
         return carry
 
-    lax.fori_loop(0, nc, first, 0)
-    for j in range(C_SLOTS):
-        c_copy(0, j)[1].start()
-    use_end(0)
+    lax.fori_loop(0, nc // 2 - 1, first_two, 0)
+    for n in range(C_SLOTS):
+        c_copy(0, n)[1].start()
+    first(nc - 2, ys0, ys1)
+    mul_last(0, a_wait(0, nc - 1), ys1)
+    a_next(0, nc - 1)
     attention()
     for j in range(B_SLOTS):
-        b_copy(0, j)[1].start()
+        b_copy(0, j)[1].start(priority=1)
+    pl.semaphore_wait(barrier, 2)
 
     for layer in range(num_layers):
         window(2 * layer, functools.partial(make_out, layer), functools.partial(use, 2 * layer + 1))
-        use_end(2 * layer + 1)
         if layer + 1 < num_layers:
             window(2 * layer + 1, functools.partial(make_down, layer), functools.partial(use, 2 * layer + 2))
-            use_end(2 * layer + 2)
             attention()
         else:
-            window(2 * layer + 1, functools.partial(make_down, layer), lambda j: out_copy(j).start())
+            window(2 * layer + 1, functools.partial(make_down, layer), lambda j: out_copy(j).start(), False)
 
     def last(j, carry):
         out_copy(j).wait()
@@ -290,27 +334,30 @@
         wq = jnp.transpose(w_qkv, (0, 2, 3, 1, 4)).reshape(num_layers, heads * 3 // 2, 2, dim, hd)
         wo = w_out.reshape(num_layers, heads * hd, dim)
         any_spec = pl.BlockSpec(memory_space=pl.ANY)
-        vmem_spec = pl.BlockSpec(memory_space=pltpu.VMEM)
         return pl.pallas_call(
             functools.partial(layer_kernel, num_layers, seq, dim, heads, hd, ffn),
             out_shape=jax.ShapeDtypeStruct((seq, dim), BF16),
-            in_specs=[any_spec] * 5 + [vmem_spec] * 2,
+            in_specs=[any_spec] * 7,
             out_specs=any_spec,
             scratch_shapes=[
+                pltpu.VMEM((num_layers, dim), F32),
+                pltpu.VMEM((num_layers, dim), F32),
                 pltpu.VMEM((nc, seq, WID), BF16),
-                pltpu.VMEM((seq + 16, ffn), F32),
+                pltpu.VMEM((seq + GAIN, ffn), F32),
                 pltpu.VMEM((seq, ffn), BF16),
                 pltpu.VMEM((nc, seq, WID), BF16),
                 pltpu.VMEM((2, nc, seq // 2, WID), BF16),
                 pltpu.VMEM((nc, seq // 2, WID), BF16),
                 pltpu.VMEM((2, nc, seq // 2, WID), BF16),
-                pltpu.VMEM((seq + 16, WID), BF16),
+                pltpu.VMEM((seq + GAIN, WID), BF16),
+                pltpu.VMEM((seq + GAIN, WID), BF16),
                 pltpu.VMEM((seq, 128), F32),
                 pltpu.VMEM((seq, 128), F32),
                 pltpu.VMEM((seq, 128), F32),
                 pltpu.VMEM((A_SLOTS, ffn // 256, WID, 256), BF16),
                 pltpu.VMEM((B_SLOTS, ffn, WID), BF16),
                 pltpu.VMEM((C_SLOTS, heads * hd, WID), BF16),
+                pltpu.SemaphoreType.DMA((2,)),
                 pltpu.SemaphoreType.DMA((nc,)),
                 pltpu.SemaphoreType.DMA((A_SLOTS,)),
                 pltpu.SemaphoreType.DMA((B_SLOTS,)),

time: 180 us -> 170 us (0.944)
  Pallas kernels: 176 us -> 165 us
    pallas_call x1, Pallas kernels: 176 us -> 165 us  [device_fn(): pl.pallas_call(functools.partial(layer_kernel, num_layers, seq, dim, head...]
where the time goes in v2:
time: 170 us; the launch traced here: 169 us
  Pallas kernels  165 us (97%)
  local copies, waits for them, and re-layouts  3.4 us (2%)
    pallas_call x1, Pallas kernels, device_fn(): pl.pallas_call(functools.partial(layer_kernel, num_layers, seq, dim, head...  165 us
    unnamed x1, local copies, waits for them, and re-layouts  3.4 us

profile of v2, /device:TPU:0, one launch (start us, length us, event | category | flops | bytes accessed | tf_op | source)
XLA Modules:
  0.0 168.8 jit_solution(2412591437301023656)
XLA Ops:
  0.0 165.3 %layers.1 = bf16[256,5120]{1,0:T(8,128)(2,1)} custom-call(bf16[256,5120]{1,0:T(8,128)(2,1)} %x_hbm.1, bf16[2,15,2,5120,128]{4,3,2,1,0:T(8,128)(2,1)} %bitcast.1.wqkv, bf16[2,1280,5120]{2,1,0:T(8,128)(2,1)} %bitcast.4, bf16[2,5120,5120]{2,1,0:T(8,128)(2,1)} %w1.1, bf16[2,5120,5120]{2,1,0:T(8,128)(2,1)} %w2.1, f32[2,5120]{1,0:T(2,128)} %g1_hbm.1, f32[2,5120]{1,0:T(2,128)} %g2_hbm.1), custom_call_target="tpu_custom_call" | custom-call | tf_op jit(solution)/shard_map/layers/pallas_call | solution.py:337
  165.4 3.4 %copy.9 = bf16[256,5120]{1,0:T(8,128)(2,1)} copy(bf16[256,5120]{1,0:T(8,128)(2,1)} %layers.1) | data formatting | bytes 5242880

commit v3 on v2

--- a/solution.py
+++ b/solution.py
@@ -20,10 +20,10 @@
 
 def layer_kernel(
     num_layers, seq, dim, heads, hd, ffn,
-    x_hbm, wqkv, wo, w1, w2, g1_hbm, g2_hbm, out_hbm,
+    x_hbm, wqkv, wo, w1, w2, g1_hbm, g2_hbm, out_ref,
     g1_ref, g2_ref, xs, acc, hid, part, recv_a, send_c, recv_c, ys0, ys1, mean0, sum1, sum2,
     a_buf, b_buf, c_buf,
-    g_sem, x_sem, a_sem, b_sem, c_sem, o_sem, sa, ra, sc, rc, sd, rd,
+    g_sem, x_sem, a_sem, b_sem, c_sem, sa, ra, sc, rc, sd, rd,
 ):
     dp = lax.axis_index("dp")
     tp = lax.axis_index("tp")
@@ -47,8 +47,8 @@
     def x_copy(j):
         return pltpu.make_async_copy(x_hbm.at[:, rows(j)], xs.at[j], x_sem.at[j])
 
-    def out_copy(j):
-        return pltpu.make_async_copy(xs.at[j], out_hbm.at[:, rows(j)], o_sem.at[j])
+    def put_out(j):
+        out_ref[:, rows(j)] = xs[j]
 
     def a_start(stage, j):
         layer, is_up = stage // 2, stage % 2
@@ -56,13 +56,10 @@
             return
         slot = lax.rem(stage * nc + j, A_SLOTS)
         if is_up:
-            def one(t, carry):
-                cols = pl.ds(pl.multiple_of(t * 256, 256), 256)
+            for t in range(up_tiles):
                 pltpu.make_async_copy(
-                    w1.at[layer, rows(j), cols], a_buf.at[slot, t], a_sem.at[slot]
+                    w1.at[layer, rows(j), pl.ds(t * 256, 256)], a_buf.at[slot, t], a_sem.at[slot]
                 ).start(priority=1)
-                return carry
-            lax.fori_loop(0, up_tiles, one, 0)
         else:
             for s in range(2):
                 pltpu.make_async_copy(
@@ -135,17 +132,19 @@
         extra = jnp.where(row == 0, hi, jnp.where(row == 1, lo, 0.0))
         y_ref[0:GAIN, :] = extra.astype(BF16)
 
-    def mul(stage, slot, y_ref):
+    def mul(stage, slot, y_ref, piece=slice(None)):
         lhs = y_ref[...]
-        for t in range(up_tiles if stage % 2 else qkv_tiles):
+        for t in range(up_tiles if stage % 2 else qkv_tiles)[piece]:
             cols = slice(t * 256, (t + 1) * 256)
             acc[:, cols] += jnp.dot(lhs, a_buf[slot, t], preferred_element_type=F32)
 
     def mul_last(stage, slot, y_ref):
-        is_up = stage % 2
+        layer, is_up = stage // 2, stage % 2
         delta = jnp.sum(sum1[...], axis=1, keepdims=True) * (1.0 / dim)
         var = jnp.sum(sum2[...], axis=1, keepdims=True) * (1.0 / dim) - delta * delta
         rstd = lax.rsqrt(jnp.maximum(var, 0.0) + 1e-5)
+        if is_up:
+            rstd = 0.5 * rstd
         back = delta * rstd
         lhs = y_ref[...]
         for t in range(up_tiles if is_up else qkv_tiles):
@@ -154,27 +153,27 @@
             colsum = full[0:1] + full[1:2]
             val = full[GAIN:] * rstd - back * colsum
             if is_up:
-                inner = val * (GELU_A + GELU_B * (val * val))
-                hv = 0.5 * val
-                val = hv + hv * jnp.tanh(inner)
+                inner = val * (2.0 * GELU_A + 8.0 * GELU_B * (val * val))
+                val = val + val * jnp.tanh(inner)
             hid[:, cols] = val.astype(BF16)
 
-    def use(stage, j):
+    def use_first(stage, j):
         @pl.when(j == 0)
         def _():
             prep_start(j)
 
         prep(stage, j, ys0)
-        slot = a_wait(stage, j)
-
-        @pl.when(j < nc - 1)
-        def _():
-            mul(stage, slot, ys0)
-
-        @pl.when(j == nc - 1)
-        def _():
-            mul_last(stage, slot, ys0)
-
+        mul(stage, a_wait(stage, j), ys0, slice(0, up_tiles // 2) if stage % 2 else slice(None))
+        if stage % 2 == 0:
+            a_next(stage, j)
+
+    def use_second(stage, j):
+        mul(stage, lax.rem(stage * nc + j, A_SLOTS), ys0, slice(up_tiles // 2, None))
+        a_next(stage, j)
+
+    def use_last(stage, j):
+        prep(stage, j, ys0)
+        mul_last(stage, a_wait(stage, j), ys0)
         a_next(stage, j)
 
     def attention():
@@ -206,7 +205,7 @@
         part[j] = jnp.dot(hid[...], b_buf[slot], preferred_element_type=F32).astype(BF16)
         ring_next(b_copy, B_SLOTS, 1, layer, j)
 
-    def window(index, make, consume, zero_acc=True):
+    def window(index, make, stage):
         par = index % 2
 
         def a_send(j):
@@ -233,6 +232,12 @@
             a_send(j).wait_recv()
             send_c[j] = (part[j, mine, :].astype(F32) + recv_a[par, j].astype(F32)).astype(BF16)
             c_send(j).start()
+
+        def finish(j):
+            a_send(j).wait_send()
+            c_send(j).wait_send()
+            d_send(j).wait_send()
+            d_recv(j).wait_recv()
 
         def step(i, carry):
             @pl.when(i < nc)
@@ -242,13 +247,20 @@
 
             @pl.when(i == 0)
             def _():
-                if zero_acc:
+                if stage is not None:
                     acc[...] = jnp.zeros_like(acc)
                 pair_sum(0)
 
             @pl.when(jnp.logical_and(i >= 2, i < nc + 1))
             def _():
                 pair_sum(i - 1)
+
+            used = i - LAG_USE
+            if stage is not None and stage % 2:
+                @pl.when(jnp.logical_and(used >= 0, used < nc - 1))
+                def _():
+                    finish(used)
+                    use_first(stage, used)
 
             @pl.when(jnp.logical_and(i >= LAG_X, i < nc + LAG_X))
             def _():
@@ -258,14 +270,24 @@
                 xs[j, mine, :] = (xs[j, mine, :].astype(F32) + total).astype(BF16)
                 d_send(j).start()
 
-            @pl.when(i >= LAG_USE)
-            def _():
-                j = i - LAG_USE
-                a_send(j).wait_send()
-                c_send(j).wait_send()
-                d_send(j).wait_send()
-                d_recv(j).wait_recv()
-                consume(j)
+            if stage is not None:
+                @pl.when(jnp.logical_and(used >= 0, used < nc - 1))
+                def _():
+                    if stage % 2:
+                        use_second(stage, used)
+                    else:
+                        finish(used)
+                        use_first(stage, used)
+
+                @pl.when(used == nc - 1)
+                def _():
+                    finish(used)
+                    use_last(stage, used)
+            else:
+                @pl.when(used >= 0)
+                def _():
+                    finish(used)
+                    put_out(used)
             return carry
 
         lax.fori_loop(0, nc + LAG_USE, step, 0)
@@ -311,18 +333,12 @@
     pl.semaphore_wait(barrier, 2)
 
     for layer in range(num_layers):
-        window(2 * layer, functools.partial(make_out, layer), functools.partial(use, 2 * layer + 1))
+        window(2 * layer, functools.partial(make_out, layer), 2 * layer + 1)
         if layer + 1 < num_layers:
-            window(2 * layer + 1, functools.partial(make_down, layer), functools.partial(use, 2 * layer + 2))
+            window(2 * layer + 1, functools.partial(make_down, layer), 2 * layer + 2)
             attention()
         else:
-            window(2 * layer + 1, functools.partial(make_down, layer), lambda j: out_copy(j).start(), False)
-
-    def last(j, carry):
-        out_copy(j).wait()
-        return carry
-
-    lax.fori_loop(0, nc, last, 0)
+            window(2 * layer + 1, functools.partial(make_down, layer), None)
 
 
 def solution(mesh):
@@ -336,9 +352,9 @@
         any_spec = pl.BlockSpec(memory_space=pl.ANY)
         return pl.pallas_call(
             functools.partial(layer_kernel, num_layers, seq, dim, heads, hd, ffn),
-            out_shape=jax.ShapeDtypeStruct((seq, dim), BF16),
+            out_shape=pltpu.VMEM((seq, dim), BF16),
             in_specs=[any_spec] * 7,
-            out_specs=any_spec,
+            out_specs=pl.BlockSpec(memory_space=pltpu.VMEM),
             scratch_shapes=[
                 pltpu.VMEM((num_layers, dim), F32),
                 pltpu.VMEM((num_layers, dim), F32),
@@ -363,7 +379,6 @@
                 pltpu.SemaphoreType.DMA((B_SLOTS,)),
                 pltpu.SemaphoreType.DMA((C_SLOTS,)),
                 pltpu.SemaphoreType.DMA((nc,)),
-                pltpu.SemaphoreType.DMA((nc,)),
                 pltpu.SemaphoreType.DMA((2, nc)),
                 pltpu.SemaphoreType.DMA((nc,)),
                 pltpu.SemaphoreType.DMA((2, nc)),
@@ -371,7 +386,7 @@
                 pltpu.SemaphoreType.DMA((2, nc)),
             ],
             compiler_params=pltpu.CompilerParams(
-                collective_id=0, has_side_effects=True, vmem_limit_bytes=67_000_000),
+                collective_id=0, has_side_effects=True, vmem_limit_bytes=62_000_000),
             name="layers",
         )(act_in, wq, wo, w_up, w_down, gain_one, gain_two)
 

time: 170 us -> 164 us (0.965)
  Pallas kernels: 165 us -> 162 us
  local copies, waits for them, and re-layouts: 3.4 us -> 1.49 us
    pallas_call x1, Pallas kernels: 165 us -> 162 us  [device_fn(): pl.pallas_call(functools.partial(layer_kernel, num_layers, seq, dim, head...]
    unnamed x1, local copies, waits for them, and re-layouts: 3.4 us -> 1.49 us
where the time goes in v3:
time: 164 us; the launch traced here: 163 us
  Pallas kernels  162 us (99%)
    pallas_call x1, Pallas kernels, device_fn(): pl.pallas_call(functools.partial(layer_kernel, num_layers, seq, dim, head...  162 us

profile of v3, /device:TPU:0, one launch (start us, length us, event | category | flops | bytes accessed | tf_op | source)
XLA Modules:
  0.0 163.3 jit_solution(8494326926626572895)
XLA Ops:
  0.0 161.8 %layers.1 = bf16[256,5120]{1,0:T(8,128)(2,1)S(1)} custom-call(bf16[256,5120]{1,0:T(8,128)(2,1)} %x_hbm.1, bf16[2,15,2,5120,128]{4,3,2,1,0:T(8,128)(2,1)} %bitcast.1.wqkv, bf16[2,1280,5120]{2,1,0:T(8,128)(2,1)} %bitcast.4, bf16[2,5120,5120]{2,1,0:T(8,128)(2,1)} %w1.1, bf16[2,5120,5120]{2,1,0:T(8,128)(2,1)} %w2.1, f32[2,5120]{1,0:T(2,128)} %g1_hbm.1, ...), custom_call_target="tpu_custom_call" | custom-call | tf_op jit(solution)/shard_map/layers/pallas_call | solution.py:353
  161.8 1.5 copy.9

commit v4 on v3

--- a/solution.py
+++ b/solution.py
@@ -132,11 +132,12 @@
         extra = jnp.where(row == 0, hi, jnp.where(row == 1, lo, 0.0))
         y_ref[0:GAIN, :] = extra.astype(BF16)
 
-    def mul(stage, slot, y_ref, piece=slice(None)):
+    def mul(stage, slot, y_ref, piece=slice(None), fresh=False):
         lhs = y_ref[...]
         for t in range(up_tiles if stage % 2 else qkv_tiles)[piece]:
             cols = slice(t * 256, (t + 1) * 256)
-            acc[:, cols] += jnp.dot(lhs, a_buf[slot, t], preferred_element_type=F32)
+            term = jnp.dot(lhs, a_buf[slot, t], preferred_element_type=F32)
+            acc[:, cols] = term if fresh else acc[:, cols] + term
 
     def mul_last(stage, slot, y_ref):
         layer, is_up = stage // 2, stage % 2
@@ -163,8 +164,12 @@
             prep_start(j)
 
         prep(stage, j, ys0)
-        mul(stage, a_wait(stage, j), ys0, slice(0, up_tiles // 2) if stage % 2 else slice(None))
-        if stage % 2 == 0:
+        slot = a_wait(stage, j)
+        if stage % 2:
+            mul(stage, slot, ys0, slice(0, up_tiles // 2))
+        else:
+            pl.when(j == 0)(lambda: mul(stage, slot, ys0, fresh=True))
+            pl.when(j > 0)(lambda: mul(stage, slot, ys0))
             a_next(stage, j)
 
     def use_second(stage, j):
@@ -205,8 +210,19 @@
         part[j] = jnp.dot(hid[...], b_buf[slot], preferred_element_type=F32).astype(BF16)
         ring_next(b_copy, B_SLOTS, 1, layer, j)
 
+    def make_down_half(layer, n):
+        slot = lax.rem(layer * nc, B_SLOTS)
+        if n == 0:
+            b_copy(layer, 0)[1].wait()
+        cols = slice(n * WID // 2, (n + 1) * WID // 2)
+        for lo in (0, half):
+            block = slice(lo, lo + half)
+            part[0, block, cols] = jnp.dot(
+                hid[block, :], b_buf[slot, :, cols], preferred_element_type=F32).astype(BF16)
+
     def window(index, make, stage):
         par = index % 2
+        layer, halved = index // 2, index % 2 == 1
 
         def a_send(j):
             return pltpu.make_async_remote_copy(
@@ -227,6 +243,22 @@
             return pltpu.make_async_remote_copy(
                 xs.at[j, other], xs.at[j, other], sd.at[j], rd.at[par, j],
                 device_id=sib, device_id_type=MESH)
+
+        def a_half(n):
+            cols = pl.ds(n * WID // 2, WID // 2)
+            return pltpu.make_async_remote_copy(
+                part.at[0, other, cols], recv_a.at[par, 0, :, cols], sa.at[0], ra.at[par, n * nc],
+                device_id=sib, device_id_type=MESH)
+
+        def half_sum(n):
+            cols = slice(n * WID // 2, (n + 1) * WID // 2)
+            a_half(n).wait_recv()
+            total = part[0, mine, cols].astype(F32) + recv_a[par, 0, :, cols].astype(F32)
+            send_c[0, :, cols] = total.astype(BF16)
+            cols = pl.ds(n * WID // 2, WID // 2)
+            pltpu.make_async_remote_copy(
+                send_c.at[0, :, cols], recv_c.at[par, 0, :, cols], sc.at[0], rc.at[par, 0],
+                device_id=pair, device_id_type=MESH).start()
 
         def pair_sum(j):
             a_send(j).wait_recv()
@@ -240,16 +272,31 @@
             d_recv(j).wait_recv()
 
         def step(i, carry):
-            @pl.when(i < nc)
+            if halved:
+                @pl.when(i == 0)
+                def _():
+                    make_down_half(layer, 0)
+                    a_half(0).start()
+
+                @pl.when(i == 0)
+                def _():
+                    make_down_half(layer, 1)
+                    a_half(1).start()
+                    ring_next(b_copy, B_SLOTS, 1, layer, 0)
+                    half_sum(0)
+
+            @pl.when(jnp.logical_and(i >= halved, i < nc))
             def _():
                 make(i)
                 a_send(i).start()
 
-            @pl.when(i == 0)
-            def _():
-                if stage is not None:
+            if halved:
+                pl.when(i == 1)(lambda: half_sum(1))
+            else:
+                @pl.when(i == 0)
+                def _():
                     acc[...] = jnp.zeros_like(acc)
-                pair_sum(0)
+                    pair_sum(0)
 
             @pl.when(jnp.logical_and(i >= 2, i < nc + 1))
             def _():
@@ -379,7 +426,7 @@
                 pltpu.SemaphoreType.DMA((B_SLOTS,)),
                 pltpu.SemaphoreType.DMA((C_SLOTS,)),
                 pltpu.SemaphoreType.DMA((nc,)),
-                pltpu.SemaphoreType.DMA((2, nc)),
+                pltpu.SemaphoreType.DMA((2, nc + 1)),
                 pltpu.SemaphoreType.DMA((nc,)),
                 pltpu.SemaphoreType.DMA((2, nc)),
                 pltpu.SemaphoreType.DMA((nc,)),

time: 164 us -> 163 us (level)
  no operation moved by 1% of the time
where the time goes in v4:
time: 163 us; the launch traced here: 162 us
  Pallas kernels  161 us (99%)
    pallas_call x1, Pallas kernels, device_fn(): pl.pallas_call(functools.partial(layer_kernel, num_layers, seq, dim, head...  161 us

profile of v4, /device:TPU:0, one launch (start us, length us, event | category | flops | bytes accessed | tf_op | source)
XLA Modules:
  0.0 162.1 jit_solution(10317236807665641030)
XLA Ops:
  0.0 160.6 %layers.1 = bf16[256,5120]{1,0:T(8,128)(2,1)S(1)} custom-call(bf16[256,5120]{1,0:T(8,128)(2,1)} %x_hbm.1, bf16[2,15,2,5120,128]{4,3,2,1,0:T(8,128)(2,1)} %bitcast.1.wqkv, bf16[2,1280,5120]{2,1,0:T(8,128)(2,1)} %bitcast.4, bf16[2,5120,5120]{2,1,0:T(8,128)(2,1)} %w1.1, bf16[2,5120,5120]{2,1,0:T(8,128)(2,1)} %w2.1, f32[2,5120]{1,0:T(2,128)} %g1_hbm.1, ...), custom_call_target="tpu_custom_call" | custom-call | tf_op jit(solution)/shard_map/layers/pallas_call | solution.py:400
  160.6 1.5 copy.9
